TPU v7x, 512 devices: a whole 4x4x16 slice. The times are simulated.
512 devices in a mesh: fsdp: 128 (over x, z, core), grp: 4 (over y).
Axes of the slice: x: 4, y: 4, z: 16, core: 2. Of those that a mesh axis runs over, the one named last changes fastest.
Arguments:
- grad: bfloat16 [28672, 8192], P('fsdp', 'grp'), may hold values from -6 to 6
- projector_t: bfloat16 [1024, 8192], P('fsdp', 'grp'), may hold values from -0.0625 to 0.0625
- first_moment: float32 [28672, 1024], P('fsdp', 'grp'), may hold values from -3 to 3
- second_moment: float32 [28672, 1024], P('fsdp', 'grp'), may hold values from 0.0001 to 0.01
Outputs:
- update: float32 [28672, 8192], P('fsdp', 'grp')
- first_new: float32 [28672, 1024], P('fsdp', 'grp')
- second_new: float32 [28672, 1024], P('fsdp', 'grp')
All inputs are finite; a program needn't handle non-finite values.
Results may differ from a plain program's by a relative error of at most 0.0029.
Values may be sent and summed in bfloat16 or wider, within the bound.
No kernel may reach another device: no remote copies, remote signals or barrier semaphores. Data moves between devices by JAX's collectives and lax.ppermute only.
A program may use at most 64 MiB of HBM per device.

v0:
```python
import jax
import jax.numpy as jnp
from jax import lax
from jax.sharding import Mesh
from jax.sharding import PartitionSpec as P

STEP = 10
FSDP = ("fsdp_0", "fsdp_1", "fsdp_2")


def joined_along(parts, dim):
    parts = jnp.moveaxis(parts, 0, dim)
    dims = parts.shape
    return parts.reshape(*dims[:dim], dims[dim] * dims[dim + 1], *dims[dim + 2 :])


def all_blocks(shard, axes, turns):
    parts = shard[None]
    for k in turns:
        parts = lax.all_gather(parts, axes[k], axis=0, tiled=True)
    carried = [lax.axis_size(axes[k]) for k in reversed(turns)]
    parts = parts.reshape(*carried, *shard.shape)
    turned = sorted(range(len(turns)), key=lambda place: turns[len(turns) - 1 - place])
    return parts.transpose(*turned, *range(len(turns), parts.ndim)).reshape(-1, *shard.shape)


def gathered_by_axis(shard, axes, turns, dim):
    return joined_along(all_blocks(shard, axes, turns), dim)


def cut_along(shard, dim, peers):
    before, after = (shard.shape[:dim], shard.shape[dim + 1 :])
    return jnp.moveaxis(shard.reshape(*before, peers, -1, *after), dim, 0)


def sum_at_owner(shard, axis, dim):
    peers = lax.axis_size(axis)
    parts = lax.all_to_all(cut_along(shard, dim, peers), axis, 0, 0, tiled=True)
    return jnp.sum(parts, axis=0)


def sent_to_all(shard, axis):
    peers = lax.axis_size(axis)
    return lax.all_to_all(
        jnp.broadcast_to(shard[None], (peers, *shard.shape)), axis, 0, 0, tiled=True
    )


def gathered_copies(shard, axis, dim):
    return joined_along(sent_to_all(shard, axis), dim)


def body(grad, projector_t, first_moment, second_moment):
    whole = gathered_by_axis(projector_t, FSDP, (0, 1, 2), 0)
    partial_value = lax.dot_general(
        grad, whole, (((1,), (1,)), ((), ())), preferred_element_type=jnp.float32
    )
    projected = sum_at_owner(partial_value, "grp", 1)
    first_new = 0.9 * first_moment + 0.1 * projected
    second_new = 0.999 * second_moment + 0.001 * projected * projected
    correct_one = 1.0 - 0.9**STEP
    correct_two = 1.0 - 0.999**STEP
    normalized = (first_new / correct_one / (jnp.sqrt(second_new / correct_two) + 1e-08)).astype(
        jnp.bfloat16
    )
    full_step = gathered_copies(normalized, "grp", 1)
    update = jnp.dot(full_step, whole, preferred_element_type=jnp.float32)
    return (update, first_new, second_new)


def solution(mesh):
    finer = Mesh(
        mesh.devices.reshape(4, 16, 2, mesh.shape["grp"]), ("fsdp_0", "fsdp_1", "fsdp_2", "grp")
    )
    return jax.shard_map(
        body,
        mesh=finer,
        in_specs=(P(FSDP, "grp"), P(FSDP, "grp"), P(FSDP, "grp"), P(FSDP, "grp")),
        out_specs=(P(FSDP, "grp"), P(FSDP, "grp"), P(FSDP, "grp")),
        check_vma=False,
    )
```

profile of v0, /device:TPU:2, one launch (start us, length us, event | category | flops | bytes accessed | tf_op | source)
XLA Modules:
  0.0 167.7 jit_solution(2398962709173067980)
XLA Ops:
  7.2 0.0 copy-start
  7.2 0.0 all-gather.4.cloned.1.call-start
  7.2 17.1 %all-gather = bf16[32,2048]{1,0:T(8,128)(2,1)} all-gather(bf16[8,2048]{1,0:T(8,128)(2,1)} %param.5), channel_id=2, replica_groups=mesh['fsdp_0'=4,'fsdp_1'=16,'fsdp_2'=2,'grp'=4] {'fsdp_0'}, dimensions={0}, use_global_device_ids=true | all-gather | bytes 163840 | tf_op jit(solution)/shard_map/all_gather | solution.py:20
  24.3 0.0 all-gather.4.cloned.1.call-update
  24.3 0.0 all-gather.6.cloned.1.call-start
  24.4 72.9 %all-gather.4.cloned.1.call-done = bf16[64,8,2048]{2,1,0:T(8,128)(2,1)} async-done(((bf16[4,8,2048]{2,1,0:T(8,128)(2,1)}), bf16[64,8,2048]{2,1,0:T(8,128)(2,1)}) %all-gather.4.cloned.1.call-update) | async-done | bytes 2097168 | tf_op jit(solution)/shard_map/all_gather | solution.py:20
  97.3 0.0 all-gather.6.cloned.1.call-update
  97.3 23.1 %all-gather.6.cloned.1.call-done = bf16[128,8,2048]{2,1,0:T(8,128)(2,1)} async-done(((bf16[64,8,2048]{2,1,0:T(8,128)(2,1)}), bf16[128,8,2048]{2,1,0:T(8,128)(2,1)}) %all-gather.6.cloned.1.call-update) | async-done | bytes 4194320 | tf_op jit(solution)/shard_map/all_gather | solution.py:20
  120.4 2.5 %copy.10 = bf16[4,16,2,8,2048]{4,3,2,1,0:T(8,128)(2,1)S(1)} copy(bf16[4,16,2,8,2048]{4,3,0,1,2:T(8,128)(2,1)} %bitcast.19) | data formatting | bytes 8388608 | tf_op jit(solution)/shard_map/transpose | solution.py:24
  122.9 0.0 copy-start.1
  122.9 1.9 %copy-done.1 = bf16[4,16,2,8,2048]{4,3,2,1,0:T(8,128)(2,1)} copy-done((bf16[4,16,2,8,2048]{4,3,2,1,0:T(8,128)(2,1)}, bf16[4,16,2,8,2048]{4,3,2,1,0:T(8,128)(2,1)S(1)}, u32[]{:S(2)}) %copy-start.1) | copy-done | bytes 4194328
  124.9 0.0 copy-done
  124.9 0.0 copy-start.2
  124.9 0.0 copy-start.3
  124.9 1.4 convolution_bitcast_fusion
  126.3 18.2 %all_to_all.10 = f32[4,224,256]{2,1,0:T(8,128)S(1)} all-to-all(f32[4,224,256]{2,1,0:T(8,128)S(1)} %convolution_bitcast_fusion), channel_id=1, replica_groups=mesh['fsdp_0'=4,'fsdp_1'=16,'fsdp_2'=2,'grp'=4] {'grp'}, dimensions={0} | all-to-all | bytes 1835008 | tf_op jit(solution)/shard_map/all_to_all | solution.py:38
  144.5 0.1 reduce_sum.9
  144.6 0.0 copy-done.2
  144.6 0.0 copy-done.3
  144.6 0.9 divide_convert_fusion
  145.5 10.8 %all_to_all.11 = bf16[4,224,256]{2,1,0:T(8,128)(2,1)S(1)} all-to-all(bf16[4,224,256]{2,1,0:T(8,128)(2,1)S(1)} %broadcast_in_dim.10), channel_id=1, replica_groups=mesh['fsdp_0'=4,'fsdp_1'=16,'fsdp_2'=2,'grp'=4] {'grp'}, dimensions={0} | all-to-all | bytes 917504 | tf_op jit(solution)/shard_map/all_to_all | solution.py:44
  156.3 4.6 %fusion.3 = f32[224,2048]{1,0:T(8,128)} fusion(bf16[224,1024]{1,0:T(8,128)(2,1)S(1)} %bitcast.20, bf16[1024,2048]{1,0:T(8,128)(2,1)} %bitcast.18), kind=kOutput, calls=%fused_computation.6 | convolution fusion | flops 939524096 | bytes 6488064 | tf_op jit(solution)/shard_map/dot_general | solution.py:67
  (2 shorter events, 0.1 us)
Async XLA Ops:
  7.2 117.7 %copy-start = (bf16[224,2048]{1,0:T(8,128)(2,1)S(1)}, bf16[224,2048]{1,0:T(8,128)(2,1)}, u32[]{:S(2)}) copy-start(bf16[224,2048]{1,0:T(8,128)(2,1)} %param.4) | copy-start | bytes 2752516
  7.2 90.1 %all-gather.4.cloned.1.call-start = ((), (), s32[]{:S(2)}) async-start(), calls=%async_computation.2 | async-start | bytes 2228224 | tf_op jit(solution)/shard_map/all_gather | solution.py:20
  24.3 96.1 %all-gather.6.cloned.1.call-start = ((), (), s32[]{:S(2)}) async-start(), calls=%async_computation.3 | async-start | bytes 6291456 | tf_op jit(solution)/shard_map/all_gather | solution.py:20
  122.9 1.9 %copy-start.1 = (bf16[4,16,2,8,2048]{4,3,2,1,0:T(8,128)(2,1)}, bf16[4,16,2,8,2048]{4,3,2,1,0:T(8,128)(2,1)S(1)}, u32[]{:S(2)}) copy-start(bf16[4,16,2,8,2048]{4,3,2,1,0:T(8,128)(2,1)S(1)} %copy.10) | copy-start | bytes 12582916
  124.9 19.7 %copy-start.2 = (f32[224,256]{1,0:T(8,128)S(1)}, f32[224,256]{1,0:T(8,128)}, u32[]{:S(2)}) copy-start(f32[224,256]{1,0:T(8,128)} %param.6) | copy-start | bytes 688132
  124.9 19.7 %copy-start.3 = (f32[224,256]{1,0:T(8,128)S(1)}, f32[224,256]{1,0:T(8,128)}, u32[]{:S(2)}) copy-start(f32[224,256]{1,0:T(8,128)} %param.7) | copy-start | bytes 688132
Sparse Core Ops, SparseCore 0:
  24.5 72.7 all-gather.3
  99.4 21.0 all-gather.5
where the time goes:
time: 168 us
  waiting for transfers between devices  96.1 us (57%)
  blocking collectives  46.1 us (27%)
  between operations  14.1 us (8%)
  matrix products  5.97 us (4%)
  local copies, waits for them, and re-layouts  4.51 us (3%)
    all_gather x2, waiting for transfers between devices, all_blocks(): parts = lax.all_gather(parts, axes[k], axis=0, tiled=True)  96 us
    all_to_all x1, blocking collectives, sum_at_owner(): parts = lax.all_to_all(cut_along(shard, dim, peers), axis, 0, 0, tiled=True)  18.2 us
    all_gather x1, blocking collectives, all_blocks(): parts = lax.all_gather(parts, axes[k], axis=0, tiled=True)  17.1 us
    all_to_all x1, blocking collectives, sent_to_all(): lax.all_to_all(jnp.broadcast_to(shard[None], (peers, *shard.shape)), axis...  10.8 us
    dot_general x1, matrix products, body(): update = jnp.dot(full_step, whole, preferred_element_type=jnp.float32)  4.56 us
  transfers between devices with their start and end apart: 2, of which 2 were waited for; matrix products, arithmetic and copies ran while one was open for 0% of the time, Pallas kernels for 0%

commit v1 on v0

v1 whole, which is shorter than its diff:
```python
import jax
import jax.numpy as jnp
from jax import lax
from jax.sharding import PartitionSpec as P

STEP = 10


def body(grad, projector_t, first_moment, second_moment):
    whole = lax.all_gather(projector_t, "fsdp", axis=0, tiled=True)
    partial_value = lax.dot_general(
        grad, whole, (((1,), (1,)), ((), ())), preferred_element_type=jnp.float32
    )
    parts = jnp.moveaxis(partial_value.reshape(partial_value.shape[0], 4, -1), 1, 0)
    projected = jnp.sum(lax.all_to_all(parts, "grp", 0, 0, tiled=True), axis=0)
    first_new = 0.9 * first_moment + 0.1 * projected
    second_new = 0.999 * second_moment + 0.001 * projected * projected
    correct_one = 1.0 - 0.9**STEP
    correct_two = 1.0 - 0.999**STEP
    normalized = (first_new / correct_one / (jnp.sqrt(second_new / correct_two) + 1e-08)).astype(
        jnp.bfloat16
    )
    full_step = lax.all_to_all(
        jnp.broadcast_to(normalized[None], (4, *normalized.shape)), "grp", 0, 0, tiled=True
    )
    full_step = jnp.moveaxis(full_step, 0, 1).reshape(normalized.shape[0], -1)
    update = jnp.dot(full_step, whole, preferred_element_type=jnp.float32)
    return (update, first_new, second_new)


def solution(mesh):
    spec = P("fsdp", "grp")
    return jax.shard_map(
        body, mesh=mesh, in_specs=(spec,) * 4, out_specs=(spec,) * 3, check_vma=False
    )
```

time: 168 us -> 203 us (1.21)
  the two profiles are of different devices: /device:TPU:2 before, /device:TPU:32 now
where the time goes in v1:
time: 203 us; the launch traced here: 202 us
  waiting for transfers between devices  150 us (74%)
  blocking collectives  29 us (14%)
  between operations  14.1 us (7%)
  matrix products  8.16 us (4%)
    all_gather x1, waiting for transfers between devices, body(): whole = lax.all_gather(projector_t, 'fsdp', axis=0, tiled=True)  149 us
    all_to_all x1, blocking collectives, body(): projected = jnp.sum(lax.all_to_all(parts, 'grp', 0, 0, tiled=True), axis=0)  18.3 us
    all_to_all x1, blocking collectives, body(): lax.all_to_all(jnp.broadcast_to(normalized[None], (4, *normalized.shape))...  10.7 us
    dot_general x1, matrix products, body(): update = jnp.dot(full_step, whole, preferred_element_type=jnp.float32)  4.56 us
  transfers between devices with their start and end apart: 1, of which 1 were waited for; matrix products, arithmetic and copies ran while one was open for 0% of the time, Pallas kernels for 0%

profile of v1, /device:TPU:32, one launch (start us, length us, event | category | flops | bytes accessed | tf_op | source)
XLA Modules:
  0.0 202.3 jit_solution(15323934384898234366)
XLA Ops:
  7.2 0.0 copy-start
  7.2 0.0 all-gather.2.cloned.1.call-start
  7.2 0.7 all-gather.2.cloned.1.call-update
  7.9 149.2 %all-gather.2.cloned.1.call-done = bf16[1024,2048]{1,0:T(8,128)(2,1)} async-done(((bf16[8,2048]{1,0:T(8,128)(2,1)}), bf16[1024,2048]{1,0:T(8,128)(2,1)}) %all-gather.2.cloned.1.call-update) | async-done | bytes 4194320 | tf_op jit(solution)/shard_map/all_gather | solution.py:10
  157.1 0.0 copy-done
  157.1 3.6 %fusion.2 = f32[224,1024]{1,0:T(8,128)S(1)} fusion(bf16[224,2048]{1,0:T(8,128)(2,1)S(1)} %copy-done, bf16[1024,2048]{1,0:T(8,128)(2,1)} %all-gather.2.cloned.1.call-done), kind=kOutput, calls=%fused_computation.5 | convolution fusion | flops 939524096 | bytes 6029312 | tf_op jit(solution)/shard_map/dot_general | solution.py:11
  160.7 0.0 copy-start.1
  160.7 0.0 copy-start.2
  160.8 0.1 copy.12
  160.8 18.3 %all_to_all.10 = f32[4,224,256]{2,1,0:T(8,128)S(1)} all-to-all(f32[4,224,256]{2,1,0:T(8,128)S(1)} %bitcast.14), channel_id=1, replica_groups=mesh['fsdp'=128,'grp'=4] {'grp'}, dimensions={0} | all-to-all | bytes 1835008 | tf_op jit(solution)/shard_map/all_to_all | solution.py:15
  179.1 0.1 reduce_sum.9
  179.2 0.0 copy-done.1
  179.2 0.0 copy-done.2
  179.2 0.9 divide_convert_fusion
  180.1 10.7 %all_to_all.11 = bf16[4,224,256]{2,1,0:T(8,128)(2,1)S(1)} all-to-all(bf16[4,224,256]{2,1,0:T(8,128)(2,1)S(1)} %broadcast_in_dim.2), channel_id=1, replica_groups=mesh['fsdp'=128,'grp'=4] {'grp'}, dimensions={0} | all-to-all | bytes 917504 | tf_op jit(solution)/shard_map/all_to_all | solution.py:23
  190.9 4.6 %fusion.3 = f32[224,2048]{1,0:T(8,128)} fusion(bf16[224,1024]{1,0:T(8,128)(2,1)S(1)} %bitcast.15, bf16[1024,2048]{1,0:T(8,128)(2,1)} %all-gather.2.cloned.1.call-done), kind=kOutput, calls=%fused_computation.6 | convolution fusion | flops 939524096 | bytes 6488064 | tf_op jit(solution)/shard_map/dot_general | solution.py:27
  (2 shorter events, 0.1 us)
Async XLA Ops:
  7.2 150.0 %copy-start = (bf16[224,2048]{1,0:T(8,128)(2,1)S(1)}, bf16[224,2048]{1,0:T(8,128)(2,1)}, u32[]{:S(2)}) copy-start(bf16[224,2048]{1,0:T(8,128)(2,1)} %param.4) | copy-start | bytes 2752516
  7.2 149.9 %all-gather.2.cloned.1.call-start = ((), (), s32[]{:S(2)}) async-start(), calls=%async_computation.2 | async-start | bytes 4227072 | tf_op jit(solution)/shard_map/all_gather | solution.py:10
  160.7 18.5 %copy-start.1 = (f32[224,256]{1,0:T(8,128)S(1)}, f32[224,256]{1,0:T(8,128)}, u32[]{:S(2)}) copy-start(f32[224,256]{1,0:T(8,128)} %param.6) | copy-start | bytes 688132
  160.7 18.5 %copy-start.2 = (f32[224,256]{1,0:T(8,128)S(1)}, f32[224,256]{1,0:T(8,128)}, u32[]{:S(2)}) copy-start(f32[224,256]{1,0:T(8,128)} %param.7) | copy-start | bytes 688132
Sparse Core Ops, SparseCore 0:
  11.1 145.9 all-gather.1

commit v2 on v1

v2 whole, which is shorter than its diff:
```python
import jax
import jax.numpy as jnp
from jax import lax
from jax.sharding import Mesh
from jax.sharding import PartitionSpec as P

STEP = 10
FSDP = ("x", "z", "c")


def copies(shard, axis):
    peers = lax.axis_size(axis)
    return lax.all_to_all(
        jnp.broadcast_to(shard[None], (peers, *shard.shape)), axis, 0, 0, tiled=True
    )


def body(grad, projector_t, first_moment, second_moment):
    parts = copies(projector_t, "z")
    parts = copies(parts, "x")
    parts = copies(parts, "c")
    whole = parts.transpose(1, 2, 0, 3, 4)
    blocks = whole.reshape(4, 256, -1)
    partial_value = lax.dot_general(
        blocks, grad, (((2,), (1,)), ((), ())), preferred_element_type=jnp.float32
    ).transpose(0, 2, 1)
    projected = jnp.sum(lax.all_to_all(partial_value, "y", 0, 0, tiled=True), axis=0)
    first_new = 0.9 * first_moment + 0.1 * projected
    second_new = 0.999 * second_moment + 0.001 * projected * projected
    correct_one = 1.0 - 0.9**STEP
    correct_two = 1.0 - 0.999**STEP
    normalized = (first_new / correct_one / (jnp.sqrt(second_new / correct_two) + 1e-08)).astype(
        jnp.bfloat16
    )
    full_step = jnp.moveaxis(copies(normalized, "y"), 0, 1).reshape(normalized.shape[0], -1)
    update = jnp.dot(full_step, whole.reshape(1024, -1), preferred_element_type=jnp.float32)
    return (update, first_new, second_new)


def solution(mesh):
    finer = Mesh(mesh.devices.reshape(4, 16, 2, 4), ("x", "z", "c", "y"))
    spec = P(FSDP, "y")
    return jax.shard_map(
        body, mesh=finer, in_specs=(spec,) * 4, out_specs=(spec,) * 3, check_vma=False
    )
```

time: 203 us -> 118 us (0.58)
  waiting for transfers between devices: 150 us -> 0 us
  blocking collectives: 29 us -> 105 us
  between operations: 14.1 us -> 0.72 us
  local copies, waits for them, and re-layouts: 0.16 us -> 4.26 us
  matrix products: 8.16 us -> 5.97 us
    all_gather x1 -> x0, waiting for transfers between devices: 149 us -> none  [body(): whole = lax.all_gather(projector_t, 'fsdp', axis=0, tiled=True)]
    all_to_all x2 -> x5, blocking collectives: 29 us -> 105 us  [the longest x4 87.2 us: copies(): lax.all_to_all(jnp.broadcast_to(shard[None], (peers, *shard.shape)), axis...]
    dot_general x2, matrix products: 8.16 us -> 5.97 us  [the longest x1 4.56 us: body(): jnp.dot(full_step, whole.reshape(1024, -1), preferred_element_type=jnp.fl...]
  transfers between devices with their start and end apart: 1 -> 0, of which waited for: 1 -> 0; matrix products, arithmetic and copies ran while one was open for 0% -> 0% of each run, Pallas kernels for 0% -> 0%
where the time goes in v2:
time: 118 us; the launch traced here: 117 us
  blocking collectives  105 us (89%)
  matrix products  5.97 us (5%)
  local copies, waits for them, and re-layouts  4.26 us (4%)
    all_to_all x4, blocking collectives, copies(): lax.all_to_all(jnp.broadcast_to(shard[None], (peers, *shard.shape)), axis...  87.2 us
    all_to_all x1, blocking collectives, body(): lax.all_to_all(partial_value, 'y', 0, 0, tiled=True)  18.3 us
    dot_general x1, matrix products, body(): jnp.dot(full_step, whole.reshape(1024, -1), preferred_element_type=jnp.fl...  4.56 us

profile of v2, /device:TPU:32, one launch (start us, length us, event | category | flops | bytes accessed | tf_op | source)
XLA Modules:
  0.0 117.3 jit_solution(9563928420059079844)
XLA Ops:
  0.6 0.0 copy-start
  0.6 0.9 broadcast_in_dim.8
  1.5 43.5 %all_to_all.25 = bf16[16,8,2048]{2,1,0:T(8,128)(2,1)S(1)} all-to-all(bf16[16,8,2048]{2,1,0:T(8,128)(2,1)S(1)} %broadcast_in_dim.8), channel_id=1, replica_groups=mesh['x'=4,'z'=16,'c'=2,'y'=4] {'z'}, dimensions={0} | all-to-all | bytes 1048576 | tf_op jit(solution)/shard_map/all_to_all | solution.py:13
  45.0 0.2 broadcast_in_dim.9
  45.3 26.3 %all_to_all.26 = bf16[4,16,8,2048]{3,2,1,0:T(8,128)(2,1)S(1)} all-to-all(bf16[4,16,8,2048]{3,2,1,0:T(8,128)(2,1)S(1)} %broadcast_in_dim.9), channel_id=1, replica_groups=mesh['x'=4,'z'=16,'c'=2,'y'=4] {'x'}, dimensions={0} | all-to-all | bytes 4194304 | tf_op jit(solution)/shard_map/all_to_all | solution.py:13
  71.5 0.5 broadcast_in_dim.10
  72.1 7.1 %all_to_all.27 = bf16[2,4,16,8,2048]{4,3,2,1,0:T(8,128)(2,1)S(1)} all-to-all(bf16[2,4,16,8,2048]{4,3,2,1,0:T(8,128)(2,1)S(1)} %broadcast_in_dim.10), channel_id=1, replica_groups=mesh['x'=4,'z'=16,'c'=2,'y'=4] {'c'}, dimensions={0} | all-to-all | bytes 8388608 | tf_op jit(solution)/shard_map/all_to_all | solution.py:13
  79.2 0.6 copy.9
  79.8 0.0 copy-start.1
  79.8 1.9 %copy-done.1 = bf16[2,4,16,8,2048]{4,3,0,2,1:T(8,128)(2,1)} copy-done((bf16[2,4,16,8,2048]{4,3,0,2,1:T(8,128)(2,1)}, bf16[2,4,16,8,2048]{4,3,0,2,1:T(8,128)(2,1)S(1)}, u32[]{:S(2)}) %copy-start.1) | copy-done | bytes 4194328
  81.7 0.0 copy-done
  81.7 0.0 copy-start.2
  81.7 0.0 copy-start.3
  81.7 1.4 %convolution_bitcast_fusion = f32[4,224,256]{2,1,0:T(8,128)S(1)} fusion(bf16[4,256,2048]{2,1,0:T(8,128)(2,1)S(1)} %bitcast.16, bf16[224,2048]{1,0:T(8,128)(2,1)S(1)} %copy-done), kind=kOutput, calls=%fused_computation | convolution fusion | flops 939524096 | bytes 6029312 | tf_op jit(solution)/shard_map/dot_general | solution.py:24
  83.1 18.3 %all_to_all.28 = f32[4,224,256]{2,1,0:T(8,128)S(1)} all-to-all(f32[4,224,256]{2,1,0:T(8,128)S(1)} %convolution_bitcast_fusion), channel_id=1, replica_groups=mesh['x'=4,'z'=16,'c'=2,'y'=4] {'y'}, dimensions={0} | all-to-all | bytes 1835008 | tf_op jit(solution)/shard_map/all_to_all | solution.py:27
  101.4 0.1 reduce_sum.9
  101.5 0.0 copy-done.2
  101.5 0.0 copy-done.3
  101.5 0.9 divide_convert_fusion
  102.4 10.3 %all_to_all.29 = bf16[4,224,256]{2,1,0:T(8,128)(2,1)S(1)} all-to-all(bf16[4,224,256]{2,1,0:T(8,128)(2,1)S(1)} %broadcast_in_dim.11), channel_id=1, replica_groups=mesh['x'=4,'z'=16,'c'=2,'y'=4] {'y'}, dimensions={0} | all-to-all | bytes 917504 | tf_op jit(solution)/shard_map/all_to_all | solution.py:13
  112.8 4.6 %fusion.3 = f32[224,2048]{1,0:T(8,128)} fusion(bf16[224,1024]{1,0:T(8,128)(2,1)S(1)} %bitcast.18, bf16[1024,2048]{1,0:T(8,128)(2,1)} %bitcast.17), kind=kOutput, calls=%fused_computation.6 | convolution fusion | flops 939524096 | bytes 6488064 | tf_op jit(solution)/shard_map/dot_general | solution.py:36
  (2 shorter events, 0.1 us)
Async XLA Ops:
  0.6 81.1 %copy-start = (bf16[224,2048]{1,0:T(8,128)(2,1)S(1)}, bf16[224,2048]{1,0:T(8,128)(2,1)}, u32[]{:S(2)}) copy-start(bf16[224,2048]{1,0:T(8,128)(2,1)} %param.4) | copy-start | bytes 2752516
  79.8 1.9 %copy-start.1 = (bf16[2,4,16,8,2048]{4,3,0,2,1:T(8,128)(2,1)}, bf16[2,4,16,8,2048]{4,3,0,2,1:T(8,128)(2,1)S(1)}, u32[]{:S(2)}) copy-start(bf16[2,4,16,8,2048]{4,3,0,2,1:T(8,128)(2,1)S(1)} %copy.9) | copy-start | bytes 12582916
  81.7 19.7 %copy-start.2 = (f32[224,256]{1,0:T(8,128)S(1)}, f32[224,256]{1,0:T(8,128)}, u32[]{:S(2)}) copy-start(f32[224,256]{1,0:T(8,128)} %param.6) | copy-start | bytes 688132
  81.7 19.8 %copy-start.3 = (f32[224,256]{1,0:T(8,128)S(1)}, f32[224,256]{1,0:T(8,128)}, u32[]{:S(2)}) copy-start(f32[224,256]{1,0:T(8,128)} %param.7) | copy-start | bytes 688132
